TPU v7x, 16 devices: a whole 2x2x2 slice. The times are simulated.
16 devices in a mesh: tp: 2 (over z), dp: 8 (over y, x, core).
Axes of the slice: x: 2, y: 2, z: 2, core: 2. Of those that a mesh axis runs over, the one named last changes fastest.
Arguments:
- hidden: bfloat16 [8, 256, 2048], P('dp')
- targets: int32 [8, 256], P('dp')
- weights: float32 [8, 256], P('dp')
- embedding: bfloat16 [49152, 2048], P('tp')
- ln_scale: float32 [2048], replicated
Outputs:
- output 1: float32 [], replicated
- output 2: bfloat16 [8, 256, 2048], P('dp')
- output 3: float32 [49152, 2048], P('tp')
- output 4: float32 [2048], replicated
All inputs are finite; a program needn't handle non-finite values.
Results may differ from a plain program's by a relative error of at most 0.001.
Values sent between devices are 32-bit elements.
A program may use at most 1.25 GiB of HBM per device.

v0:
```python
import jax
import jax.numpy as jnp
from jax import lax
from jax.sharding import PartitionSpec as P

LN_EPS = 1e-6
Z_WEIGHT = 1e-4


def solution(mesh):
    dp_size = mesh.shape["dp"]

    def local_step(hidden, targets, weights, embedding, ln_scale):
        vocab_local = embedding.shape[0]
        token_count = hidden.shape[0] * hidden.shape[1] * dp_size
        vocab_start = lax.axis_index("tp") * vocab_local
        h_float = hidden.astype(jnp.float32)
        centered = h_float - jnp.mean(h_float, -1, keepdims=True)
        inv_std = lax.rsqrt(jnp.mean(centered * centered, -1, keepdims=True) + LN_EPS)
        x_hat = centered * inv_std
        h_norm = (x_hat * ln_scale).astype(jnp.bfloat16)
        logits = jnp.einsum("bte,ve->btv", h_norm, embedding, preferred_element_type=jnp.float32)
        row_max = lax.pmax(jnp.max(logits, -1, keepdims=True), "tp")
        vocab_ids = vocab_start + lax.broadcasted_iota(jnp.int32, (1, 1, vocab_local), 2)
        is_target = vocab_ids == targets[:, :, None]
        local_stats = jnp.concatenate([jnp.sum(jnp.exp(logits - row_max), -1, keepdims=True), jnp.sum(jnp.where(is_target, logits, 0.0), -1, keepdims=True)], axis=-1)
        tp_stats = lax.psum(local_stats, "tp")
        log_z = row_max + jnp.log(tp_stats[:, :, 0:1])
        tgt_logit = tp_stats[:, :, 1:2]
        total_w = lax.psum(jnp.sum(weights), "dp")
        loss_tok = (log_z - tgt_logit + Z_WEIGHT * log_z * log_z)[:, :, 0]
        mean_loss = lax.psum(jnp.sum(weights * loss_tok), "dp") / total_w
        tok_coef = (weights * (token_count / total_w))[:, :, None]
        soft_prob = jnp.exp(logits - log_z)
        d_logits = ((soft_prob * (1.0 + 2.0 * Z_WEIGHT * log_z) - jnp.where(is_target, 1.0, 0.0)) * tok_coef).astype(jnp.bfloat16)
        d_hn = lax.psum(jnp.einsum("btv,ve->bte", d_logits, embedding, preferred_element_type=jnp.float32), "tp")
        d_emb = lax.psum(jnp.einsum("btv,bte->ve", d_logits, h_norm, preferred_element_type=jnp.float32), "dp")
        value_a6 = d_hn * ln_scale
        d_hidden = inv_std * (value_a6 - jnp.mean(value_a6, -1, keepdims=True) - x_hat * jnp.mean(value_a6 * x_hat, -1, keepdims=True))
        d_ln = lax.psum(jnp.sum(d_hn * x_hat, axis=(0, 1)), "dp")
        return mean_loss, d_hidden.astype(jnp.bfloat16), d_emb, d_ln

    return jax.shard_map(local_step, mesh=mesh, in_specs=(P("dp", None, None), P("dp", None), P("dp", None), P("tp", None), P(None)), out_specs=(P(), P("dp", None, None), P("tp", None), P(None)), check_vma=False)
```

profile of v0, /device:TPU:0, one launch (start us, length us, event | category | flops | bytes accessed | tf_op | source)
XLA Modules:
  0.0 2546.5 jit_solution(8775468510022126383)
XLA Ops:
  7.2 0.0 all-reduce.4.cloned.1.call-start
  7.2 1.4 convert_reduce_fusion
  8.7 1.6 fusion.16
  10.3 0.0 copy-start.1
  10.4 45.1 %fusion.29 = (f32[256]{0:T(256)S(1)}, f32[256,24576]{1,0:T(8,128)}) fusion(bf16[24576,2048]{1,0:T(8,128)(2,1)} %param.8, bf16[1,256,2048]{2,1,0:T(8,128)(2,1)} %param.5, f32[2048]{0:T(1024)} %param.9, f32[256]{0:T(256)S(1)} %add_rsqrt_fusion, f32[256]{0:T(256)S(1)} %broadcast_multiply_fusion.3), kind=kOutput, calls=%fused_computation.43 | convolution fusion | flops 25778716672 | bytes 126888960 | tf_op jit(solution)/shard_map/bte,ve->btv/dot_general | solution.py:22
  55.5 6.2 pmax.7
  61.7 12.2 exponential_reduce_fusion
  73.9 4.9 psum.42
  78.8 0.6 fusion.27
  79.4 12.4 psum.44
  92.6 0.0 copy-start
  92.6 0.0 copy-start.2
  92.6 44.7 %convolution_bitcast_fusion = f32[1,256,2048]{2,1,0:T(8,128)} fusion(bf16[24576,2048]{1,0:T(8,128)(2,1)} %param.8, f32[256,24576]{1,0:T(8,128)} %get-tuple-element.16, f32[256]{0:T(256)S(1)} %bitcast.34, f32[256]{0:T(256)S(1)} %bitcast.32, f32[256]{0:T(256)S(1)} %bitcast.30, s32[24576]{0:T(1024)S(1)} %iota_add_fusion, s32[256]{0:T(256)S(1)} %bitcast.37), kind=kOutput, calls=%fused_computation.7 | convolution fusion | flops 25813843968 | bytes 128028672 | tf_op jit(solution)/shard_map/btv,ve->bte/dot_general | solution.py:36
  137.3 0.0 all-reduce.4.cloned.1.call-update
  137.3 0.2 all-reduce.6.cloned.1.call-start
  137.6 0.0 copy-done
  137.6 74.2 %fusion.21 = f32[24576,2048]{1,0:T(8,128)} fusion(bf16[1,256,2048]{2,1,0:T(8,128)(2,1)S(1)} %copy-done, f32[2048]{0:T(1024)S(1)} %copy-done.2, f32[256]{0:T(256)S(1)} %add_rsqrt_fusion, f32[256]{0:T(256)S(1)} %broadcast_multiply_fusion.3, f32[256,24576]{1,0:T(8,128)} %get-tuple-element.16, f32[256]{0:T(256)S(1)} %bitcast.35, f32[256]{0:T(256)S(1)} %bitcast.33, ...), kind=kOutput, calls=%fused_computation.40 | convolution fusion | flops 25816465408 | bytes 227653632 | tf_op jit(solution)/shard_map/btv,bte->ve/dot_general | solution.py:37
  211.8 0.0 all-reduce.6.cloned.1.call-update
  211.8 0.0 all-reduce.4.cloned.1.call-done
  211.9 2.5 fusion.15
  214.4 14.6 all-reduce
  230.3 3.3 fusion.14
  233.6 2175.7 %all-reduce.6.cloned.1.call-done = f32[24576,2048]{1,0:T(8,128)} async-done(((f32[24576,2048]{1,0:T(8,128)}), f32[24576,2048]{1,0:T(8,128)}) %all-reduce.6.cloned.1.call-update) | async-done | bytes 201326608 | tf_op jit(solution)/shard_map/psum | solution.py:37
  2409.3 129.2 %copy.11 = f32[24576,2048]{1,0:T(8,128)} copy(f32[24576,2048]{1,0:T(8,128)} %all-reduce.6.cloned.1.call-done) | data formatting | bytes 402653184
  (11 shorter events, 0.1 us)
Async XLA Ops:
  7.2 204.7 %all-reduce.4.cloned.1.call-start = ((), (), s32[]{:S(2)}) async-start(), calls=%async_computation | async-start | bytes 4194304 | tf_op jit(solution)/shard_map/psum | solution.py:36
  10.3 51.3 %copy-start.1 = (s32[1,256]{1,0:T(1,128)S(1)}, s32[1,256]{1,0:T(1,128)}, u32[]{:S(2)}) copy-start(s32[1,256]{1,0:T(1,128)} %param.6) | copy-start | bytes 3076
  61.7 17.1 copy-start.3
  92.6 45.0 %copy-start = (bf16[1,256,2048]{2,1,0:T(8,128)(2,1)S(1)}, bf16[1,256,2048]{2,1,0:T(8,128)(2,1)}, u32[]{:S(2)}) copy-start(bf16[1,256,2048]{2,1,0:T(8,128)(2,1)} %param.5) | copy-start | bytes 3145732
  92.6 45.0 %copy-start.2 = (f32[2048]{0:T(1024)S(1)}, f32[2048]{0:T(1024)}, u32[]{:S(2)}) copy-start(f32[2048]{0:T(1024)} %param.9) | copy-start | bytes 24580
  137.3 2271.9 %all-reduce.6.cloned.1.call-start = ((), (), s32[]{:S(2)}) async-start(), calls=%async_computation.1 | async-start | bytes 402653184 | tf_op jit(solution)/shard_map/psum | solution.py:37
Sparse Core Ops, SparseCore 0:
  137.4 59.5 all-reduce.3
  212.0 2197.2 all-reduce.5
where the time goes:
time: 2550 us
  waiting for transfers between devices  2180 us (85%)
  matrix products  164 us (6%)
  local copies, waits for them, and re-layouts  129 us (5%)
  blocking collectives  38.2 us (1%)
    psum x1, waiting for transfers between devices, local_step(): lax.psum(jnp.einsum('btv,bte->ve', d_logits, h_norm, preferred_element_ty...  2180 us
    unnamed x9, local copies, waits for them, and re-layouts  129 us
    dot_general x1, matrix products, local_step(): jnp.einsum('btv,bte->ve', d_logits, h_norm, preferred_element_type=jnp.fl...  74.2 us
  transfers between devices with their start and end apart: 2, of which 1 were waited for; matrix products, arithmetic and copies ran while one was open for 3% of the time, Pallas kernels for 0%

commit v1 on v0

v1 whole, which is shorter than its diff:
```python
import functools

import jax
import jax.numpy as jnp
from jax import lax
from jax.experimental import pallas as pl
from jax.experimental.pallas import tpu as pltpu
from jax.sharding import PartitionSpec as P

LN_EPS = 1e-6
Z_WEIGHT = 1e-4
LOG2E = 1.4426950408889634
LN2 = 0.6931471805599453
MESH = pl.DeviceIdType.MESH
F32 = jnp.float32
BF16 = jnp.bfloat16

S = 256
E = 2048
S2 = S + S
LANE = 128
VT = 24576
VH = VT // 2
NSEQ = 8
NTOK = NSEQ * S
BUCKETS = (768, 1024, 1280, 1536, 2048)
ALIGN = 8

VBA = 2048
NBA = VH // VBA
LNR = 64

VB1 = 512
SLOTS = 5
GROUP, SENT, TURN = 12, 11, 13
VB2 = 512

NT = (((1,), (1,)), ((), ()))
NN = (((1,), (0,)), ((), ()))


def _flip(dp, k):
    out = dp
    for bit in (1, 2, 4):
        if k & bit:
            out = out + bit * (1 - 2 * lax.rem(dp // bit, 2))
    return out


def _dev(tp, dp, z, k):
    return {"tp": tp + z * (1 - 2 * tp), "dp": _flip(dp, k)}


def _remote(src, dst, ss, rs, dev):
    return pltpu.make_async_remote_copy(src_ref=src, dst_ref=dst, send_sem=ss, recv_sem=rs, device_id=dev, device_id_type=MESH)


def _to_cols(rows8):
    return jnp.transpose(jnp.concatenate([rows8, jnp.zeros((120, rows8.shape[1]), F32)], axis=0))


def _places(w):
    i0 = lax.broadcasted_iota(jnp.int32, (S, S), 0)
    i1 = lax.broadcasted_iota(jnp.int32, (S, S), 1)
    flags = jnp.broadcast_to(jnp.where(w > 0.0, 1.0, 0.0), (8, S)).astype(BF16)
    pos = jnp.dot(flags, jnp.where(i0 < i1, 1.0, 0.0).astype(BF16), preferred_element_type=F32)[0:1]
    return jnp.where(w > 0.0, pos, -1.0)


def _norm(xf):
    cen = xf - jnp.mean(xf, axis=-1, keepdims=True)
    inv = lax.rsqrt(jnp.mean(cen * cen, axis=-1, keepdims=True) + LN_EPS)
    return cen * inv, inv


def _front(x_ref, w_ref, y_ref, g_ref, emb_ref, gath_ref, stats_ref, own_ref, sib_ref, dln_ref, cnt_ref, which_ref,
           hnf, xh, hn2, lg, ebuf, dlbuf, acc, m_s, s_s, t_s, bz, bb, by, wyc, wy_all, st4,
           e_sem, l_sem, row_ss, row_rs, wy_ss, wy_rs, st_ss, st_rs, sq_ss, sq_rs):
    tp = lax.axis_index("tp")
    dp = lax.axis_index("dp")
    core = lax.rem(dp, 2)
    sib = _flip(dp, 1)
    dpx, dpy, dpd = _flip(dp, 2), _flip(dp, 4), _flip(dp, 6)
    here = tp * 2 + core
    bar = pltpu.get_barrier_semaphore()
    for k in range(1, 8):
        pl.semaphore_signal(bar, inc=1, device_id=_dev(tp, dp, 0, k), device_id_type=MESH)
    for k in (0, 1):
        pl.semaphore_signal(bar, inc=1, device_id=_dev(tp, dp, 1, k), device_id_type=MESH)

    def emb_copy(j):
        row = pl.multiple_of(core * VH + j * VBA, VBA)
        slot = lax.rem(j, 2)
        return pltpu.make_async_copy(emb_ref.at[pl.ds(row, VBA)], ebuf.at[slot], e_sem.at[slot])

    emb_copy(0).start()
    i0 = lax.broadcasted_iota(jnp.int32, (S, S), 0)
    hit = i0 == _places(w_ref[...]).astype(jnp.int32)
    xc, xc_sib = acc.at[0:S], acc.at[S:S2]
    xc[...] = jnp.dot(jnp.where(hit, 1.0, 0.0).astype(BF16), x_ref[...], preferred_element_type=F32)
    wc = jnp.sum(jnp.where(hit, w_ref[...], 0.0), axis=1, keepdims=True)
    yc = jnp.sum(jnp.where(hit, y_ref[...].astype(F32), 0.0), axis=1, keepdims=True)
    ln = lax.broadcasted_iota(jnp.int32, (S, LANE), 1)
    wyc[...] = jnp.transpose(jnp.where(ln == 0, wc, jnp.where(ln == 1, yc, 0.0)))[0:8, :]
    wy_all[dp] = wyc[...]

    def layer_norm(src, half, keep):
        @pl.loop(0, S // LNR)
        def _(r):
            rows = pl.ds(pl.multiple_of(r * LNR, LNR), LNR)
            at = pl.ds(pl.multiple_of(half * S + r * LNR, LNR), LNR)
            h, _ = _norm(src[rows, :])
            xh[at, :] = h
            b = (h * g_ref[...]).astype(BF16)
            hn2[at, :] = b
            if keep:
                hnf[rows, :] = b.astype(F32)

    layer_norm(xc, core, True)
    pl.semaphore_wait(bar, 9)

    def rcopy(k, src, dst, dev):
        return _remote(src, dst, row_ss.at[k], row_rs.at[k], dev)

    Q = S // 4

    def quarter(k, part=0, parts=1):
        q = k + tp * (3 - 2 * k)
        return pl.ds(pl.multiple_of(q * Q + part * (Q // parts), 8), Q // parts)

    to_x, to_y, to_sib, to_z = _dev(tp, dp, 0, 2), _dev(tp, dp, 0, 4), _dev(tp, dp, 0, 1), _dev(tp, dp, 1, 0)
    x_cp = rcopy(0, xc, xc_sib, to_sib)

    def onward(k, q, rows, dev):
        return rcopy(k, gath_ref.at[q, rows], gath_ref.at[q, rows], dev)

    ex = [rcopy(1 + k, hnf.at[quarter(k)], gath_ref.at[dp, quarter(k)], to_x) for k in range(3)]
    ey = [rcopy(4 + k, hnf.at[quarter(k)], gath_ref.at[dp, quarter(k)], to_y) for k in range(3)]
    d0, d1 = onward(7, dpx, quarter(0), to_y), onward(8, dpy, quarter(1), to_x)
    d2, d3 = onward(9, dpx, quarter(2, 0, 2), to_y), onward(10, dpy, quarter(2, 1, 2), to_x)
    zx, zy, zd = (onward(11 + i, q, quarter(0), to_z) for i, q in enumerate((dpx, dpy, dpd)))
    fx, fy, fd = ([onward(14 + 4 * i + k, q, quarter(k), to_sib) for k in range(4)] for i, q in enumerate((dpx, dpy, dpd)))
    f_own = onward(26, dp, pl.ds(0, S), to_sib)
    wy_cp = [_remote(wyc, wy_all.at[dp], wy_ss.at[k], wy_rs.at[k], _dev(tp, dp, 0, k)) for k in range(1, 8)]
    x_cp.start()
    for c in wy_cp:
        c.start()

    for c in (ex[0], ey[1], ex[1], ey[0]):
        c.start()
    own_cp = pltpu.make_async_copy(hnf, gath_ref.at[dp], l_sem.at[0])
    own_cp.start()
    for c in wy_cp:
        c.wait()
    first = dp - core
    wrow = jnp.concatenate([wy_all[first, 0:1], wy_all[first + 1, 0:1]], axis=1)
    yrow = jnp.concatenate([wy_all[first, 1:2], wy_all[first + 1, 1:2]], axis=1)
    cols = _to_cols(jnp.broadcast_to(yrow, (8, S2)))
    by[...] = jnp.broadcast_to(cols[:, 0:1], (S2, LANE)).astype(jnp.int32)
    m_s[...] = jnp.full((S2, LANE), -1e30, F32)
    s_s[...] = jnp.zeros((S2, LANE), F32)
    t_s[...] = jnp.zeros((S2, LANE), F32)
    lane = lax.broadcasted_iota(jnp.int32, (S2, LANE), 1)
    base = tp * VT + core * VH
    x_cp.wait_recv()
    layer_norm(xc_sib, 1 - core, False)
    x_cp.wait_send()
    acc[...] = jnp.zeros((S2, E), F32)

    @pl.loop(0, NBA)
    def _(j):
        slot = lax.rem(j, 2)
        emb_copy(j).wait()

        @pl.when(j + 1 < NBA)
        def _():
            emb_copy(j + 1).start()

        @pl.when(j == 2)
        def _():
            ex[0].wait_recv()
            for c in (d0, zx):
                c.start()
            ey[1].wait_recv()
            for c in (d1, ex[2], ey[2], fx[0], fy[1]):
                c.start()

        @pl.when(j == 4)
        def _():
            ey[0].wait_recv()
            for c in (zy, fy[0]):
                c.start()
            ex[1].wait_recv()
            fx[1].start()

        l = lax.dot_general(hn2[...], ebuf[slot], NT, preferred_element_type=F32) * LOG2E
        lg[j] = l
        parts = [l[:, c * LANE:(c + 1) * LANE] for c in range(VBA // LANE)]
        mx = m_s[...]
        for p in parts:
            mx = jnp.maximum(mx, p)
        s = s_s[...] * jnp.exp2(m_s[...] - mx)
        t = t_s[...]
        yy = by[...] - (base + j * VBA)
        for c, p in enumerate(parts):
            s = s + jnp.exp2(p - mx)
            t = jnp.where(yy == lane + c * LANE, p, t)
        m_s[...] = mx
        s_s[...] = s
        t_s[...] = t

    emb_copy(0).start()
    mx = jnp.max(m_s[...], axis=1, keepdims=True)
    sm = jnp.sum(s_s[...] * jnp.exp2(m_s[...] - mx), axis=1, keepdims=True)
    tg = jnp.sum(t_s[...], axis=1, keepdims=True)
    packed = jnp.where(lane == 0, mx, jnp.where(lane == 1, sm, jnp.where(lane == 2, tg, 0.0)))
    st4[here] = jnp.transpose(packed)[0:8, :]
    st_cp = [_remote(st4.at[here], st4.at[here], st_ss.at[i], st_rs.at[i], _dev(tp, dp, z, k))
             for i, (z, k) in enumerate(((0, 1), (1, 0), (1, 1)))]
    for c in st_cp:
        c.start()
    w8 = jnp.concatenate([wy_all[q, 0:1] for q in range(NSEQ)], axis=0)
    total = jnp.sum(w8)
    start = jnp.int32(0)
    for q in range(NSEQ):
        cnt = jnp.sum(jnp.where(w8[q:q + 1] > 0.0, 1.0, 0.0)).astype(jnp.int32)
        cnt_ref[q] = cnt
        cnt_ref[NSEQ + q] = start
        start = start + (cnt + ALIGN - 1) // ALIGN * ALIGN
    which = sum((start > t).astype(jnp.int32) for t in BUCKETS[:-1])
    which_ref[0] = which
    cnt_ref[2 * NSEQ] = BUCKETS[0] // S + sum((which > i).astype(jnp.int32) * ((BUCKETS[i + 1] - BUCKETS[i]) // S) for i in range(len(BUCKETS) - 1))
    own_cp.wait()
    f_own.start()
    d0.wait_recv()
    for c in (zd, fd[0]):
        c.start()
    d1.wait_recv()
    fd[1].start()
    for c in st_cp:
        c.wait()
    ms = [st4[q, 0:1] for q in range(4)]
    mg = jnp.maximum(jnp.maximum(ms[0], ms[1]), jnp.maximum(ms[2], ms[3]))
    sg = jnp.zeros_like(mg)
    tgr = jnp.zeros_like(mg)
    for q in range(4):
        sg = sg + st4[q, 1:2] * jnp.exp2(ms[q] - mg)
        tgr = tgr + st4[q, 2:3]
    logz = (mg + jnp.log2(sg)) * LN2
    tgr = tgr * LN2
    coef_b = wrow * (jnp.full((1, S2), float(NTOK), F32) / total)
    coef_a = coef_b * (1.0 + 2.0 * Z_WEIGHT * logz)
    shift = jnp.where(coef_a > 0.0, mg + jnp.log2(sg) - jnp.log2(coef_a), 1e30)
    sub = lax.broadcasted_iota(jnp.int32, (8, S2), 0)
    rows8 = jnp.where(sub == 0, yrow, jnp.where(sub == 1, logz, jnp.where(sub == 2, shift, jnp.where(
        sub == 3, coef_b, jnp.where(sub == 4, tgr, jnp.where(sub == 5, wrow, total))))))
    stats_ref[dp] = jnp.where(core == 0, rows8[:, :S], rows8[:, S:])
    sq_cp = [_remote(stats_ref.at[dp], stats_ref.at[dp], sq_ss.at[k], sq_rs.at[k], _dev(tp, dp, 0, k)) for k in range(1, 8)]
    for c in sq_cp:
        c.start()
    cols = _to_cols(rows8)
    bz[...] = jnp.broadcast_to(cols[:, 2:3], (S2, LANE))
    bb[...] = jnp.broadcast_to(cols[:, 3:4], (S2, LANE))

    @pl.loop(0, NBA)
    def _(j):
        slot = lax.rem(j, 2)
        emb_copy(j).wait()

        @pl.when(j + 1 < NBA)
        def _():
            emb_copy(j + 1).start()

        @pl.when(j == NBA // 3)
        def _():
            ex[2].wait_recv()
            for c in (d2, fx[2]):
                c.start()
            ey[2].wait_recv()
            for c in (d3, fy[2]):
                c.start()
            zx.wait_recv()
            fx[3].start()
            zy.wait_recv()
            fy[3].start()

        @pl.when(j == NBA - 1)
        def _():
            d2.wait_recv()
            d3.wait_recv()
            fd[2].start()

        yy = by[...] - (base + j * VBA)
        z, b = bz[...], bb[...]
        for c in range(VBA // LANE):
            p = jnp.exp2(lg[j, :, c * LANE:(c + 1) * LANE] - z)
            dlbuf[:, c * LANE:(c + 1) * LANE] = jnp.where(yy == lane + c * LANE, p - b, p).astype(BF16)
        acc[...] += lax.dot_general(dlbuf[...], ebuf[slot], NN, preferred_element_type=F32)

    own_out = pltpu.make_async_copy(acc.at[pl.ds(pl.multiple_of(core * S, S), S)], own_ref, l_sem.at[0])
    sib_out = pltpu.make_async_copy(acc.at[pl.ds(pl.multiple_of((1 - core) * S, S), S)], sib_ref, l_sem.at[1])
    own_out.start()
    sib_out.start()
    zd.wait_recv()
    fd[3].start()
    dln = jnp.zeros((8, E), F32)
    for q in range(S2 // 8):
        dln = dln + acc[q * 8:(q + 1) * 8, :] * xh[q * 8:(q + 1) * 8, :]
    dln_ref[...] = jnp.sum(dln, axis=0, keepdims=True)
    for c in sq_cp:
        c.wait()
    own_out.wait()
    sib_out.wait()
    for c in ex + ey + [d0, d1, d2, d3, zx, zy, zd]:
        c.wait_send()
    for c in fx + fy + fd + [f_own]:
        c.wait()


def front(x, w, y, g, emb):
    vm = pl.BlockSpec(memory_space=pltpu.VMEM)
    hbm = pl.BlockSpec(memory_space=pl.ANY)
    dma = pltpu.SemaphoreType.DMA
    sm = pl.BlockSpec(memory_space=pltpu.SMEM)
    tile = pltpu.VMEM((S2, LANE), F32)
    seq = jax.ShapeDtypeStruct((S, E), F32)
    return pl.pallas_call(
        _front,
        out_shape=(jax.ShapeDtypeStruct((NSEQ, S, E), F32), jax.ShapeDtypeStruct((NSEQ, 8, S), F32), seq, seq,
                   jax.ShapeDtypeStruct((1, E), F32), jax.ShapeDtypeStruct((32,), jnp.int32), jax.ShapeDtypeStruct((1,), jnp.int32)),
        in_specs=[vm, vm, vm, vm, hbm], out_specs=(hbm, vm, hbm, hbm, vm, sm, sm),
        scratch_shapes=[
            pltpu.VMEM((S, E), F32), pltpu.VMEM((S2, E), F32), pltpu.VMEM((S2, E), BF16),
            pltpu.VMEM((NBA, S2, VBA), F32), pltpu.VMEM((2, VBA, E), BF16), pltpu.VMEM((S2, VBA), BF16),
            pltpu.VMEM((S2, E), F32), tile, tile, tile, tile, tile, pltpu.VMEM((S2, LANE), jnp.int32),
            pltpu.VMEM((8, S), F32), pltpu.VMEM((NSEQ, 8, S), F32), pltpu.VMEM((4, 8, S2), F32),
            dma((2,)), dma((2,)), dma((27,)), dma((27,)), dma((8,)), dma((8,)), dma((3,)), dma((3,)), dma((8,)), dma((8,)),
        ],
        compiler_params=pltpu.CompilerParams(collective_id=0, has_side_effects=True, vmem_limit_bytes=67043328),
        cost_estimate=pl.CostEstimate(flops=2 * 2 * S2 * VH * E, bytes_accessed=2 * VH * E * 2, transcendentals=0),
        name="front",
    )(x, w, y, g, emb)


def _pack(cnt_ref, stats_ref, gath_ref, hc_ref, rows_ref, loss_ref, stage, hbuf, g_sem, h_sem):
    def copy(s, k, rows):
        src = pl.ds(pl.multiple_of(k * ALIGN, ALIGN), rows)
        dst = pl.ds(pl.multiple_of(cnt_ref[NSEQ + s] + k * ALIGN, ALIGN), rows)
        return pltpu.make_async_copy(gath_ref.at[s, src], stage.at[dst], g_sem.at[s, k])

    def each(s, op):
        many = 8
        full = cnt_ref[s] // (many * ALIGN)

        @pl.loop(0, full)
        def _(k):
            op(copy(s, k * many, many * ALIGN))

        @pl.loop(full * many, (cnt_ref[s] + ALIGN - 1) // ALIGN)
        def _(k):
            op(copy(s, k, ALIGN))

    for s in range(NSEQ):
        each(s, lambda cp: cp.start())
    last = NSEQ - 1
    end = cnt_ref[NSEQ + last] + (cnt_ref[last] + ALIGN - 1) // ALIGN * ALIGN

    blocks = cnt_ref[2 * NSEQ]

    @pl.loop(end // ALIGN, blocks * (S // ALIGN))
    def _(k):
        stage[pl.ds(pl.multiple_of(k * ALIGN, ALIGN), ALIGN), :] = jnp.zeros((ALIGN, E), F32)

    lanes = lax.broadcasted_iota(jnp.int32, (8, NTOK), 1)
    rows = jnp.where(lax.broadcasted_iota(jnp.int32, (8, NTOK), 0) == 2, 1e30, 0.0)
    loss = jnp.zeros((1, S), F32)
    for s in range(NSEQ):
        st = stats_ref[s]
        wide = jnp.concatenate([st, jnp.zeros((8, NTOK - S), F32)], axis=1)
        at = cnt_ref[NSEQ + s]
        rows = jnp.where((lanes >= at) & (lanes < at + cnt_ref[s]), pltpu.roll(wide, at, axis=1), rows)
        logz, tgt, w = st[1:2], st[4:5], st[5:6]
        loss = loss + jnp.where(w > 0.0, w * (logz - tgt + Z_WEIGHT * logz * logz), 0.0)
    rows_ref[...] = rows
    loss_ref[0, 0] = jnp.sum(loss / stats_ref[0, 6:7, :])
    for s in range(NSEQ):
        each(s, lambda cp: cp.wait())

    def put(b):
        at = pl.ds(pl.multiple_of(b * S, S), S)
        return pltpu.make_async_copy(hbuf.at[at], hc_ref.at[at], h_sem.at[b])

    @pl.loop(0, blocks)
    def _(b):
        for q in range(S // 64):
            at = pl.ds(pl.multiple_of(b * S + q * 64, 64), 64)
            hbuf[at, :] = stage[at, :].astype(BF16)
        put(b).start()

    @pl.loop(0, blocks)
    def _(b):
        put(b).wait()


def pack(cnt, stats, gath):
    vm = pl.BlockSpec(memory_space=pltpu.VMEM)
    sm = pl.BlockSpec(memory_space=pltpu.SMEM)
    hbm = pl.BlockSpec(memory_space=pl.ANY)
    return pl.pallas_call(
        _pack,
        out_shape=(jax.ShapeDtypeStruct((NTOK, E), BF16), jax.ShapeDtypeStruct((8, NTOK), F32), jax.ShapeDtypeStruct((1, 1), F32)),
        in_specs=[sm, vm, hbm], out_specs=(hbm, vm, sm),
        scratch_shapes=[pltpu.VMEM((NTOK, E), F32), pltpu.VMEM((NTOK, E), BF16), pltpu.SemaphoreType.DMA((NSEQ, S // ALIGN)),
                        pltpu.SemaphoreType.DMA((NTOK // S,))],
        compiler_params=pltpu.CompilerParams(vmem_limit_bytes=60 * 1024 * 1024),
        name="pack",
    )(cnt, stats, gath)


def _tail(x_ref, w_ref, g_ref, ln_ref, d0_ref, d1_ref, d2_ref, d3_ref, out_ref, dln_ref, xc, dc):
    i0 = lax.broadcasted_iota(jnp.int32, (S, S), 0)
    dest = _places(w_ref[...])
    dln = ln_ref[0]
    for q in range(1, 16):
        dln = dln + ln_ref[q]
    dln_ref[...] = dln
    pick = jnp.where(i0 == dest.astype(jnp.int32), 1.0, 0.0).astype(BF16)
    xc[...] = jnp.dot(pick, x_ref[...], preferred_element_type=F32)

    @pl.loop(0, S // LNR)
    def _(r):
        rows = pl.ds(pl.multiple_of(r * LNR, LNR), LNR)
        h, inv = _norm(xc[rows, :])
        a = ((d0_ref[rows, :] + d1_ref[rows, :]) + (d2_ref[rows, :] + d3_ref[rows, :])) * g_ref[...]
        d = inv * (a - jnp.mean(a, axis=-1, keepdims=True) - h * jnp.mean(a * h, axis=-1, keepdims=True))
        dc[rows, :] = d.astype(BF16)

    i1 = lax.broadcasted_iota(jnp.int32, (S, S), 1)
    back = jnp.where(_to_cols(jnp.broadcast_to(dest, (8, S)))[:, 0:1].astype(jnp.int32) == i1, 1.0, 0.0).astype(BF16)
    out_ref[...] = jnp.dot(back, dc[...], preferred_element_type=F32).astype(BF16)


def tail(x, w, g, ln, parts):
    vm = pl.BlockSpec(memory_space=pltpu.VMEM)
    return pl.pallas_call(
        _tail, out_shape=(jax.ShapeDtypeStruct((S, E), BF16), jax.ShapeDtypeStruct((1, E), F32)), in_specs=[vm] * 8, out_specs=(vm, vm),
        scratch_shapes=[pltpu.VMEM((S, E), F32), pltpu.VMEM((S, E), BF16)],
        compiler_params=pltpu.CompilerParams(vmem_limit_bytes=40 * 1024 * 1024), name="tail",
    )(x, w, g, ln, *parts)


def _dlogits(n, hc_ref, rows_ref, emb_ref, part_ref, dl_ref, all16, hc, ebuf, sbuf, h_sem, e_sem, w_sem, ss, rs, p_ss, p_rs):
    tp = lax.axis_index("tp")
    dp = lax.axis_index("dp")
    core = lax.rem(dp, 2)
    sib = _flip(dp, 1)
    nblk = VH // VB1
    steps = nblk // GROUP * TURN
    bar = pltpu.get_barrier_semaphore()
    others = [(z, k) for z in (0, 1) for k in range(8) if z or k]
    for z, k in others:
        pl.semaphore_signal(bar, inc=1, device_id=_dev(tp, dp, z, k), device_id_type=MESH)

    def row_of(i):
        q, k = i // TURN, lax.rem(i, TURN)
        extra = k // GROUP
        half = core + extra * (1 - 2 * core)
        return pl.multiple_of(half * VH + (q * GROUP + k - extra) * VB1, VB1)

    def emb_copy(i):
        slot = lax.rem(i, 2)
        return pltpu.make_async_copy(emb_ref.at[pl.ds(row_of(i), VB1)], ebuf.at[slot], e_sem.at[slot])

    def out_copy(i):
        slot = lax.rem(i, SLOTS)
        return pltpu.make_async_copy(sbuf.at[slot], dl_ref.at[pl.ds(row_of(i), VB1)], w_sem.at[slot])

    def send_copy(i):
        slot = lax.rem(i, SLOTS)
        rows = pl.ds(row_of(i), VB1)
        return pltpu.make_async_remote_copy(src_ref=sbuf.at[slot], dst_ref=dl_ref.at[rows], send_sem=ss.at[slot],
                                            recv_sem=rs.at[i // TURN * SENT + lax.rem(i, TURN)], device_id={"dp": sib}, device_id_type=MESH)

    h_copy = pltpu.make_async_copy(hc_ref.at[pl.ds(0, n)], hc, h_sem)
    h_copy.start()
    emb_copy(0).start()
    me = tp * 8 + dp
    all16[me] = part_ref[...]
    pl.semaphore_wait(bar, 15)
    part_cp = [_remote(part_ref, all16.at[me], p_ss.at[z * 8 + k], p_rs.at[z * 8 + k], _dev(tp, dp, z, k)) for z, k in others]
    for c in part_cp:
        c.start()
    h_copy.wait()
    shift, coef_b = rows_ref[2:3, :n], rows_ref[3:4, :n]
    sub = lax.broadcasted_iota(jnp.int32, (VB1, n), 0)

    @pl.loop(0, steps)
    def _(i):
        slot = lax.rem(i, SLOTS)
        emb_copy(i).wait()

        @pl.when(i + 1 < steps)
        def _():
            emb_copy(i + 1).start()

        @pl.when(i >= SLOTS)
        def _():
            out_copy(i - SLOTS).wait()

            @pl.when(lax.rem(i - SLOTS, TURN) < SENT)
            def _():
                send_copy(i - SLOTS).wait_send()

        yy = rows_ref[0:1, :n].astype(jnp.int32) - (tp * VT + row_of(i))
        l = lax.dot_general(ebuf[lax.rem(i, 2)], hc[...], NT, preferred_element_type=F32)
        p = jnp.exp2(l * LOG2E - shift)
        sbuf[slot] = jnp.where(sub == yy, p - coef_b, p)
        out_copy(i).start()

        @pl.when(lax.rem(i, TURN) < SENT)
        def _():
            send_copy(i).start()

    for i in range(steps - SLOTS, steps):
        out_copy(i).wait()
        if i % TURN < SENT:
            send_copy(i).wait_send()

    @pl.loop(0, nblk // GROUP * SENT)
    def _(i):
        send_copy(i // SENT * TURN + lax.rem(i, SENT)).wait_recv()
    for c in part_cp:
        c.wait()


def dlogits(n, cid, hc, rows, emb, part):
    dma = pltpu.SemaphoreType.DMA
    vm = pl.BlockSpec(memory_space=pltpu.VMEM)
    hbm = pl.BlockSpec(memory_space=pl.ANY)
    return pl.pallas_call(
        functools.partial(_dlogits, n),
        out_shape=(jax.ShapeDtypeStruct((VT, n), F32), jax.ShapeDtypeStruct((16, 1, E), F32)),
        in_specs=[hbm, vm, hbm, vm], out_specs=(hbm, vm),
        scratch_shapes=[pltpu.VMEM((n, E), BF16), pltpu.VMEM((2, VB1, E), BF16), pltpu.VMEM((SLOTS, VB1, n), F32),
                        dma, dma((2,)), dma((SLOTS,)), dma((SLOTS,)), dma((VH // VB1 // GROUP * SENT,)), dma((16,)), dma((16,))],
        compiler_params=pltpu.CompilerParams(collective_id=cid, has_side_effects=True, vmem_limit_bytes=60 * 1024 * 1024),
        cost_estimate=pl.CostEstimate(flops=2 * VH * n * E, bytes_accessed=VH * E * 2 + 2 * VH * n * 4, transcendentals=0),
        name=f"dlogits{n}",
    )(hc, rows, emb, part)


def _demb(dl_ref, hc_ref, out_ref):
    out_ref[...] = jnp.dot(dl_ref[...].astype(BF16), hc_ref[...], preferred_element_type=F32)


def demb(n, dl, hc):
    vb = 1024 if n < 2048 else 256
    return pl.pallas_call(
        _demb, grid=(VT // vb,),
        out_shape=jax.ShapeDtypeStruct((VT, E), F32),
        in_specs=[pl.BlockSpec((vb, n), lambda i: (i, 0)), pl.BlockSpec((n, E), lambda i: (0, 0), pipeline_mode=pl.Buffered(1))],
        out_specs=pl.BlockSpec((vb, E), lambda i: (i, 0)),
        compiler_params=pltpu.CompilerParams(dimension_semantics=("arbitrary",), vmem_limit_bytes=60 * 1024 * 1024),
        cost_estimate=pl.CostEstimate(flops=2 * VT * n * E, bytes_accessed=VT * E * 4 + VT * n * 4, transcendentals=0),
        name=f"demb{n}",
    )(dl, hc)


def solution(mesh):
    swap_core = [(i, i ^ 1) for i in range(16)]
    swap_both = [(i, i ^ 9) for i in range(16)]

    def local_step(hidden, targets, weights, embedding, ln_scale):
        x = hidden[0]
        g = ln_scale[None, :]
        gath, stats, mine, other, part, cnt, which = front(x, weights, targets, g, embedding)
        from_sib = lax.ppermute(other, ("tp", "dp"), swap_core)
        from_z = lax.ppermute(mine, "tp", [(0, 1), (1, 0)])
        from_both = lax.ppermute(other, ("tp", "dp"), swap_both)
        hc, rows, loss = pack(cnt, stats, gath)

        def back_of(i, n):
            def run(hc, rows, emb, part):
                dl, ln = dlogits(n, 1 + i, hc, rows, emb, part)
                return demb(n, dl, hc), ln
            return run

        d_emb, ln = lax.switch(which[0], [back_of(i, n) for i, n in enumerate(BUCKETS)], hc, rows, embedding, part)
        d_hidden, dln = tail(x, weights, g, ln, (mine, from_sib, from_z, from_both))
        return loss[0, 0], d_hidden[None], d_emb, dln[0]

    return jax.shard_map(local_step, mesh=mesh,
                         in_specs=(P("dp", None, None), P("dp", None), P("dp", None), P("tp", None), P(None)),
                         out_specs=(P(), P("dp", None, None), P("tp", None), P(None)), check_vma=False)
```

time: 2550 us -> 340 us (0.13)
  waiting for transfers between devices: 2180 us -> 0.01 us
  Pallas kernels: 0 us -> 330 us
  matrix products: 164 us -> 0 us
  local copies, waits for them, and re-layouts: 129 us -> 0.02 us
  blocking collectives: 38.2 us -> 0 us
    psum x2 -> x0, waiting for transfers between devices: 2180 us -> none  [the longest x1 2180 us: local_step(): lax.psum(jnp.einsum('btv,bte->ve', d_logits, h_norm, preferred_element_ty...]
    pallas_call x0 -> x5, Pallas kernels: none -> 330 us  [the longest x1 141 us: demb(): pl.pallas_call(_demb, grid=(VT // vb,), out_shape=jax.ShapeDtypeStruct((V...]
    dot_general x3 -> x0, matrix products: 164 us -> none  [the longest x1 74.2 us: local_step(): jnp.einsum('btv,bte->ve', d_logits, h_norm, preferred_element_type=jnp.fl...]
    unnamed x9 -> x8, local copies, waits for them, and re-layouts: 129 us -> 0.02 us
    psum x3 -> x0, blocking collectives: 32 us -> none  [the longest x1 14.6 us: local_step(): mean_loss = lax.psum(jnp.sum(weights * loss_tok), 'dp') / total_w]
  transfers between devices with their start and end apart: 2 -> 3, of which waited for: 1 -> 0; matrix products, arithmetic and copies ran while one was open for 3% -> 0% of each run, Pallas kernels for 0% -> 72%
where the time goes in v1:
time: 340 us; the launch traced here: 337 us
  Pallas kernels  330 us (97%)
    pallas_call x1, Pallas kernels, demb(): pl.pallas_call(_demb, grid=(VT // vb,), out_shape=jax.ShapeDtypeStruct((V...  141 us
    pallas_call x1, Pallas kernels, dlogits(): pl.pallas_call(functools.partial(_dlogits, n), out_shape=(jax.ShapeDtypeS...  92.3 us
    pallas_call x1, Pallas kernels, front(): pl.pallas_call(_front, out_shape=(jax.ShapeDtypeStruct((NSEQ, S, E), F32)...  79.3 us
    pallas_call x1, Pallas kernels, pack(): pl.pallas_call(_pack, out_shape=(jax.ShapeDtypeStruct((NTOK, E), BF16), j...  10.4 us
  transfers between devices with their start and end apart: 3, of which 0 were waited for; matrix products, arithmetic and copies ran while one was open for 0% of the time, Pallas kernels for 72%

profile of v1, /device:TPU:0, one launch (start us, length us, event | category | flops | bytes accessed | tf_op | source)
XLA Modules:
  0.0 337.0 jit_solution(4665566526931525378)
XLA Ops:
  0.6 79.3 %front.1 = (f32[8,256,2048]{2,1,0:T(8,128)}, f32[8,8,256]{2,1,0:T(8,128)}, f32[256,2048]{1,0:T(8,128)}, f32[256,2048]{1,0:T(8,128)}, f32[1,2048]{1,0:T(1,128)}, /*index=5*/s32[32]{0:T(128)}, s32[1]{0:T(128)}) custom-call(bf16[256,2048]{1,0:T(8,128)(2,1)} %bitcast.6, f32[1,256]{1,0:T(1,128)} %w_ref.3, s32[1,256]{1,0:T(1,128)} %y_ref.1, f32[1,2048]{1,0:T(1,128)} %bitcast.8, ...), custom_call_target="tpu_custom_call" | custom-call | flops 51539607552 | bytes 100663296 | tf_op jit(solution)/shard_map/front/pallas_call | solution.py:327
  80.0 0.6 collective-permute-start
  80.6 0.4 collective-permute-start.1
  81.0 1.0 collective-permute-start.2
  82.0 10.4 %pack.1 = (bf16[2048,2048]{1,0:T(8,128)(2,1)}, f32[8,2048]{1,0:T(8,128)S(1)}, f32[1,1]{1,0:T(1,128)}) custom-call(s32[32]{0:T(128)} %get-tuple-element.88.cnt_ref, f32[8,8,256]{2,1,0:T(8,128)} %get-tuple-element.89.stats_ref, f32[8,256,2048]{2,1,0:T(8,128)} %get-tuple-element.90.gath_ref), custom_call_target="tpu_custom_call" | custom-call | tf_op jit(solution)/shard_map/pack/pallas_call | solution.py:409
  93.0 0.0 copy-start
  93.0 0.0 copy-start.1
  93.0 0.0 copy-start.2
  93.0 0.0 copy-start.3
  93.0 236.9 %conditional.1 = (f32[24576,2048]{1,0:T(8,128)}, f32[16,1,2048]{2,1,0:T(1,128)}) conditional(s32[]{:T(128)} %bitcast.3, (bf16[2048,2048]{1,0:T(8,128)(2,1)}, f32[8,2048]{1,0:T(8,128)S(1)}, bf16[24576,2048]{1,0:T(8,128)(2,1)}, f32[1,2048]{1,0:T(1,128)}) %tuple.28, (bf16[2048,2048]{1,0:T(8,128)(2,1)}, ...), branch_computations={%region_0.0_spmd, %region_1.0_spmd, %region_2.0_spmd, %region_3.0_... | conditional | flops 309237645312 | bytes 654311424 | solution.py:588
  94.4 92.3 %dlogits1280.1 = (f32[24576,1280]{1,0:T(8,128)}, f32[16,1,2048]{2,1,0:T(1,128)}) custom-call(bf16[2048,2048]{1,0:T(8,128)(2,1)} %get-tuple-element.52.hc_ref, f32[8,2048]{1,0:T(8,128)S(1)} %get-tuple-element.53.rows_ref, bf16[24576,2048]{1,0:T(8,128)(2,1)} %get-tuple-element.54.emb_ref, f32[1,2048]{1,0:T(1,128)} %get-tuple-element.55.part_ref), custom_call_target="tpu_custom_call" | custom-call | flops 64424509440 | bytes 176160768 | tf_op jit(solution)/shard_map/cond/branch_2_fun/dlogits1280/pallas_call | solution.py:540
  186.7 141.5 %demb1280.1 = f32[24576,2048]{1,0:T(8,128)} custom-call(f32[24576,1280]{1,0:T(8,128)} %get-tuple-element.56.dl_ref, bf16[2048,2048]{1,0:T(8,128)(2,1)} %get-tuple-element.52.hc_ref), custom_call_target="tpu_custom_call" | custom-call | flops 128849018880 | bytes 327155712 | tf_op jit(solution)/shard_map/cond/branch_2_fun/demb1280/pallas_call | solution.py:558
  329.9 0.0 collective-permute-done.d1_ref
  329.9 0.0 collective-permute-done.1.d2_ref
  329.9 0.0 collective-permute-done.2.d3_ref
  329.9 0.0 copy-done
  329.9 0.0 copy-done.1
  330.0 0.0 copy-done.2
  330.0 0.0 copy-done.3
  330.0 6.8 %tail.1 = (bf16[256,2048]{1,0:T(8,128)(2,1)}, f32[1,2048]{1,0:T(1,128)}) custom-call(bf16[256,2048]{1,0:T(8,128)(2,1)S(1)} %bitcast.7, f32[1,256]{1,0:T(1,128)S(1)} %copy-done.3, f32[1,2048]{1,0:T(1,128)S(1)} %bitcast.9, f32[16,1,2048]{2,1,0:T(1,128)} %get-tuple-element.96.ln_ref, f32[256,2048]{1,0:T(8,128)S(1)} %copy-done, ...), custom_call_target="tpu_custom_call" | custom-call | tf_op jit(solution)/shard_map/tail/pallas_call | solution.py:445
Async XLA Ops:
  80.0 249.9 %collective-permute-start = (f32[256,2048]{1,0:T(8,128)}, f32[256,2048]{1,0:T(8,128)}, u32[]{:S(2)}, u32[]{:S(2)}) collective-permute-start(f32[256,2048]{1,0:T(8,128)} %get-tuple-element.98), channel_id=1, source_target_pairs={{0,1},{1,0},{2,3},{3,2},{4,5},{5,4},{6,7},{7,6},{8,9},{9,8},{10,11... | collective-permute-start | bytes 6291464 | tf_op jit(solution)/shard_map/ppermute | solution.py:577
  80.6 249.3 %collective-permute-start.1 = (f32[256,2048]{1,0:T(8,128)}, f32[256,2048]{1,0:T(8,128)}, u32[]{:S(2)}, u32[]{:S(2)}) collective-permute-start(f32[256,2048]{1,0:T(8,128)} %get-tuple-element.97.d0_ref), channel_id=1, source_target_pairs={{0,8},{8,0},{1,9},{9,1},{2,10},{10,2},{3,11},{11,3},{4,12},{12,4},... | collective-permute-start | bytes 6291464 | tf_op jit(solution)/shard_map/ppermute | solution.py:578
  81.0 248.9 %collective-permute-start.2 = (f32[256,2048]{1,0:T(8,128)}, f32[256,2048]{1,0:T(8,128)}, u32[]{:S(2)}, u32[]{:S(2)}) collective-permute-start(f32[256,2048]{1,0:T(8,128)} %get-tuple-element.98), channel_id=1, source_target_pairs={{0,9},{1,8},{2,11},{3,10},{4,13},{5,12},{6,15},{7,14},{8,1},{9,0},... | collective-permute-start | bytes 6291464 | tf_op jit(solution)/shard_map/ppermute | solution.py:579
  93.0 237.0 %copy-start = (f32[256,2048]{1,0:T(8,128)S(1)}, f32[256,2048]{1,0:T(8,128)}, u32[]{:S(2)}) copy-start(f32[256,2048]{1,0:T(8,128)} %get-tuple-element.97.d0_ref) | copy-start | bytes 6291460
  93.0 237.0 %copy-start.1 = (bf16[1,256,2048]{2,1,0:T(8,128)(2,1)S(1)}, bf16[1,256,2048]{2,1,0:T(8,128)(2,1)}, u32[]{:S(2)}) copy-start(bf16[1,256,2048]{2,1,0:T(8,128)(2,1)} %param.10) | copy-start | bytes 3145732
  93.0 237.0 %copy-start.2 = (f32[2048]{0:T(1024)S(1)}, f32[2048]{0:T(1024)}, u32[]{:S(2)}) copy-start(f32[2048]{0:T(1024)} %param.14) | copy-start | bytes 24580
  93.0 236.9 %copy-start.3 = (f32[1,256]{1,0:T(1,128)S(1)}, f32[1,256]{1,0:T(1,128)}, u32[]{:S(2)}) copy-start(f32[1,256]{1,0:T(1,128)} %w_ref.3) | copy-start | bytes 3076
